TPU v7x, 32 devices: a whole 2x2x4 slice. The times are simulated.
32 devices in a mesh: dom: 4 (over x, core), orb: 8 (over z, y).
Axes of the slice: x: 2, y: 2, z: 4, core: 2. Of those that a mesh axis runs over, the one named last changes fastest.
Arguments:
- orbitals: float32 [4, 16, 48, 2304], P('dom', 'orb'), may hold values from -6 to 6
- occupations: float32 [4, 16], P('dom', 'orb'), may hold values from 0.25 to 2
- occupied_count: int32 [4], P('dom'), may hold values from 4 to 16
- weights: float32 [4, 48], P('dom'), may hold values from 0 to 1, as said below
- external_potential: float32 [4, 48, 2304], P('dom'), may hold values from -2 to 0.5
- core_density: float32 [4, 48, 2304], P('dom'), may hold values from 0.08 to 2.88, as said below
- hartree_guess: float32 [128, 2304], P(('dom', 'orb')), may hold values from -6 to 6
Outputs:
- potential: float32 [128, 2304], P(('dom', 'orb'))
Inputs may be any that keep to these rules, and one draw needn't show every extreme that they name: orbitals 0 to occupied_count - 1 of a domain are occupied. `weights`: positive; on every global plane the weights of the boxes that cover it sum to one. `core_density`: positive.
All inputs are finite; a program needn't handle non-finite values.
Results may differ from a plain program's by a relative error of at most 0.00017.
Values sent between devices are 32-bit elements; how exact they have to be, the bound alone decides.
A program may use at most 64 MiB of HBM per device.

v0:
```python
import functools

import jax
import jax.numpy as jnp
from jax import lax
from jax.experimental import pallas as pl
from jax.experimental.pallas import tpu as pltpu
from jax.sharding import PartitionSpec as P

SIDE = 48
CORE = 32
BUF = 8
DEGREE = 8
SWEEPS = 4
CYCLES = 2


EXCHANGE_FACTOR = (3.0 / 3.141592653589793) ** (1.0 / 3.0)
FOUR_PI = 4.0 * 3.141592653589793
RELAXATION = 0.8
CUTOFF = 1.5


def transverse_sum(field):
    cells = field.shape[-1]
    column = jnp.arange(cells, dtype=jnp.int32) % SIDE
    left = jnp.where(column == 0, jnp.roll(field, -(SIDE - 1), -1), jnp.roll(field, 1, -1))
    right = jnp.where(column == SIDE - 1, jnp.roll(field, SIDE - 1, -1), jnp.roll(field, -1, -1))
    return left + right + jnp.roll(field, SIDE, -1) + jnp.roll(field, -SIDE, -1)


def hamiltonian(orbital_set, box_potential):
    padded = jnp.pad(orbital_set, ((0, 0), (1, 1), (0, 0)))
    neighbours = padded[:, 2:] + padded[:, :-2] + transverse_sum(orbital_set)
    return 0.5 * (6.0 * orbital_set - neighbours) + box_potential[None] * orbital_set


def chebyshev(orbital_set, box_potential):
    low_bound = jnp.min(box_potential) + CUTOFF
    high_bound = jnp.max(box_potential) + 6.0
    center = 0.5 * (high_bound + low_bound)
    half_width = 0.5 * (high_bound - low_bound)
    previous = orbital_set
    current = (hamiltonian(orbital_set, box_potential) - center * orbital_set) / half_width
    for step_index in range(DEGREE - 1):
        following = (
            2.0 * (hamiltonian(current, box_potential) - center * current) / half_width - previous
        )
        previous, current = (current, following)
    return current


MESH = pl.DeviceIdType.MESH


def lane_neighbours(field, column):
    cells = field.shape[-1]
    left = jnp.where(
        column == 0, pltpu.roll(field, cells - (SIDE - 1), 1), pltpu.roll(field, 1, 1)
    )
    right = jnp.where(
        column == SIDE - 1, pltpu.roll(field, SIDE - 1, 1), pltpu.roll(field, cells - 1, 1)
    )
    return left + right + pltpu.roll(field, SIDE, 1) + pltpu.roll(field, cells - SIDE, 1)


def field_kernel(last, doms, ranks, *refs):
    weighted, start = refs[:2]
    outs = 1 if last else 2
    outputs = refs[2 : 2 + outs]
    (parts, near_h, near_d, work, work_d, own_pot, box_pot, sums, dom_sums) = refs[
        2 + outs : 11 + outs
    ]
    (
        part_send, part_recv, h_send, h_recv, d_send, d_recv,
        sum_send, sum_recv, dom_send, dom_recv, box_send, box_recv,
    ) = refs[11 + outs :]
    chunks, planes, cells = weighted.shape
    rim = BUF // planes
    reach = near_h.shape[0] // 2
    everyone = doms * ranks
    dom = lax.axis_index("dom")
    rank = lax.axis_index("orb")
    me = dom * ranks + rank
    in_low = rank < rim
    in_high = rank >= ranks - rim
    in_rim = jnp.logical_or(in_low, in_high)

    def place(index):
        return (lax.div(index, ranks), lax.rem(index, ranks))

    def send(source, target, send_sem, recv_sem, index):
        return pltpu.make_async_remote_copy(
            src_ref=source, dst_ref=target, send_sem=send_sem, recv_sem=recv_sem,
            device_id=index, device_id_type=MESH,
        )

    def repeat(low, high, step):
        lax.fori_loop(low, high, lambda i, carry: (step(i), carry)[1], 0)

    barrier = pltpu.get_barrier_semaphore()

    def greet(k):
        pl.semaphore_signal(
            barrier, inc=1, device_id=place(lax.rem(me + k, everyone)), device_id_type=MESH
        )

    repeat(1, everyone, greet)
    pl.semaphore_wait(barrier, everyone - 1)

    def part_copy(k):
        chunk = lax.rem(rank + rim + k, chunks)
        owner = lax.rem(dom * ranks + chunk - rim + everyone, everyone)
        to = place(owner)
        slot = jnp.where(to[0] == dom, rank, ranks + rank)
        return send(
            weighted.at[chunk], parts.at[slot], part_send.at[chunk], part_recv.at[slot], to
        )

    repeat(1, chunks, lambda k: part_copy(k).start())

    def near_copies(source, buffer, send_sems, recv_sems):
        copies = []
        for k in range(1, reach + 1):
            for sign in (1, -1):
                to = place(lax.rem(me + sign * k + everyone, everyone))
                slot = reach - sign * k
                copies.append(
                    send(source, buffer.at[slot], send_sems.at[slot], recv_sems.at[slot], to)
                )
        return copies

    h_copies = near_copies(start, near_h, h_send, h_recv)
    for copy in h_copies:
        copy.start()

    charge = weighted[0]
    for chunk in range(1, chunks):
        charge = charge + weighted[chunk]
    charge = jnp.sum(charge, axis=0, keepdims=True)
    row = charge[:, :128]
    for lane in range(128, cells, 128):
        row = row + charge[:, lane : lane + 128]
    sums[rank] = jnp.broadcast_to(row, (8, 128))

    def sum_copy(k):
        to = (dom, lax.rem(rank + k, ranks))
        return send(sums.at[rank], sums.at[rank], sum_send.at[k], sum_recv.at[rank], to)

    repeat(1, ranks, lambda k: sum_copy(k).start())

    def arrived(buffer, slot, sems):
        send(buffer.at[slot], buffer.at[slot], sems.at[slot], sems.at[slot], (dom, rank)).wait_recv()

    near_d[reach] = weighted[rank + rim]

    def take(slot):
        arrived(parts, slot, part_recv)
        near_d[reach] += parts[slot]

    repeat(1, ranks, lambda k: take(lax.rem(rank + k, ranks)))

    @pl.when(in_rim)
    def _():
        repeat(0, ranks, lambda k: take(ranks + lax.rem(rank + k, ranks)))

    d_copies = near_copies(near_d.at[reach], near_d, d_send, d_recv)
    for copy in d_copies:
        copy.start()

    repeat(1, ranks, lambda k: arrived(sums, lax.rem(rank + k, ranks), sum_recv))
    dom_sums[dom] = jnp.sum(sums[...], axis=0)

    def dom_copy(k):
        to = (lax.rem(dom + k, doms), rank)
        return send(dom_sums.at[dom], dom_sums.at[dom], dom_send.at[k], dom_recv.at[dom], to)

    repeat(1, doms, lambda k: dom_copy(k).start())

    work[...] = jnp.zeros_like(work)
    work_d[...] = jnp.zeros_like(work_d)
    near_h[reach] = start[...]
    for slot in range(2 * reach + 1):
        if slot != reach:
            arrived(near_h, slot, h_recv)
        work[slot * planes : (slot + 1) * planes, :] = near_h[slot]
    for slot in range(2 * reach + 1):
        if slot != reach:
            arrived(near_d, slot, d_recv)
        work_d[slot * planes : (slot + 1) * planes, :] = near_d[slot]

    field = work[...]
    source = FOUR_PI * work_d[...]
    rows = field.shape[0]
    column = lax.broadcasted_iota(jnp.int32, field.shape, 1) % SIDE
    for _ in range(SWEEPS):
        near = pltpu.roll(field, 1, 0) + pltpu.roll(field, rows - 1, 0)
        near = near + lane_neighbours(field, column)
        field = field + RELAXATION * ((near + source) * (1.0 / 6.0) - field)
    work[...] = field
    mine = work[reach * planes : (reach + 1) * planes, :]
    density = near_d[reach]
    root = jnp.exp(jnp.log(density) * (1.0 / 3.0))
    root = root - (root - density / (root * root)) * (1.0 / 3.0)
    own_pot[...] = mine - EXCHANGE_FACTOR * root

    def box_copy(k):
        to = (dom, lax.rem(rank + k, ranks))
        slot = rank + rim
        return send(own_pot, box_pot.at[slot], box_send.at[k], box_recv.at[slot], to)

    def rim_copy(k):
        to_dom = jnp.where(in_low, lax.rem(dom + doms - 1, doms), lax.rem(dom + 1, doms))
        slot = jnp.where(in_low, rank + ranks + rim, rank - ranks + rim)
        to = (to_dom, lax.rem(rank + k, ranks))
        return send(own_pot, box_pot.at[slot], box_send.at[ranks + k], box_recv.at[slot], to)

    if not last:
        repeat(1, ranks, lambda k: box_copy(k).start())

        @pl.when(in_rim)
        def _():
            repeat(0, ranks, lambda k: rim_copy(k).start())

    repeat(1, doms, lambda k: arrived(dom_sums, lax.rem(dom + k, doms), dom_recv))
    total = jnp.sum(jnp.sum(dom_sums[...], axis=0)[:1, :])
    average = total / (everyone * planes * cells)
    shift = (-SWEEPS * RELAXATION * FOUR_PI / 6.0) * average
    if last:
        outputs[0][...] = own_pot[...] + shift
    else:
        outputs[1][...] = mine + shift
        box_pot[rank + rim] = own_pot[...]
        repeat(
            1, chunks, lambda k: arrived(box_pot, lax.rem(rank + rim + k, chunks), box_recv)
        )
        outputs[0][...] = box_pot[...] + shift
        repeat(1, ranks, lambda k: box_copy(k).wait_send())

        @pl.when(in_rim)
        def _():
            repeat(0, ranks, lambda k: rim_copy(k).wait_send())

    repeat(1, chunks, lambda k: part_copy(k).wait_send())
    for copy in h_copies + d_copies:
        copy.wait_send()
    repeat(1, ranks, lambda k: sum_copy(k).wait_send())
    repeat(1, doms, lambda k: dom_copy(k).wait_send())


def field_step(weighted, hartree, last):
    doms, ranks = lax.axis_size("dom"), lax.axis_size("orb")
    planes, cells = hartree.shape
    chunks = weighted.shape[0] // planes
    reach = -(-SWEEPS // planes)
    span = 2 * reach + 1
    rows = -(-span * planes // 8) * 8
    f32 = jnp.float32
    box = jax.ShapeDtypeStruct((chunks, planes, cells), f32)
    own = jax.ShapeDtypeStruct((planes, cells), f32)
    vmem = pl.BlockSpec(memory_space=pltpu.VMEM)
    dma = pltpu.SemaphoreType.DMA
    results = pl.pallas_call(
        functools.partial(field_kernel, last, doms, ranks),
        out_shape=(own,) if last else (box, own),
        in_specs=[vmem, vmem],
        out_specs=(vmem,) if last else (vmem, vmem),
        scratch_shapes=[
            pltpu.VMEM((2 * ranks, planes, cells), f32),
            pltpu.VMEM((span, planes, cells), f32),
            pltpu.VMEM((span, planes, cells), f32),
            pltpu.VMEM((rows, cells), f32),
            pltpu.VMEM((rows, cells), f32),
            pltpu.VMEM((planes, cells), f32),
            pltpu.VMEM((chunks, planes, cells), f32),
            pltpu.VMEM((ranks, 8, 128), f32),
            pltpu.VMEM((doms, 8, 128), f32),
            dma((chunks,)), dma((2 * ranks,)),
            dma((span,)), dma((span,)),
            dma((span,)), dma((span,)),
            dma((ranks,)), dma((ranks,)),
            dma((doms,)), dma((doms,)),
            dma((2 * ranks,)), dma((chunks,)),
        ],
        compiler_params=pltpu.CompilerParams(
            collective_id=1 if last else 0, has_side_effects=True
        ),
        name="field_last" if last else "field_first",
    )(weighted.reshape(chunks, planes, cells), hartree)
    if last:
        return results[0], None
    return results[0].reshape(chunks * planes, cells), results[1]


def body(
    orbitals, occupations, occupied_count, weights, external_potential, core_density, hartree_guess
):
    orb_count = lax.axis_size("orb")
    orb_rank = lax.axis_index("orb")
    per_device = orbitals.shape[1]
    orbital_rank = orb_rank * per_device + jnp.arange(per_device, dtype=jnp.int32)
    factors = jnp.where(orbital_rank < occupied_count[0], occupations[0], jnp.float32(0.0)) / (
        per_device * orb_count
    )
    box_weight = weights[0][:, None]
    core_share = core_density[0] / orb_count
    ionic = external_potential[0]
    orbital_set = orbitals[0]
    hartree = hartree_guess
    scf_box = jnp.zeros_like(ionic)
    for cycle_index in range(CYCLES):
        orbital_set = chebyshev(orbital_set, ionic + scf_box)
        squares = jnp.mean(orbital_set * orbital_set, axis=(1, 2)) + 1e-06
        orbital_set = orbital_set / jnp.sqrt(squares)[:, None, None]
        density_part = jnp.sum(factors[:, None, None] * orbital_set * orbital_set, axis=0)
        weighted = (density_part + core_share) * box_weight
        last = cycle_index + 1 == CYCLES
        result, hartree = field_step(weighted, hartree, last)
        scf_box = result
    return result


def solution(mesh):
    placed = (
        P("dom", "orb", None, None),
        P("dom", "orb"),
        P("dom"),
        P("dom", None),
        P("dom", None, None),
        P("dom", None, None),
        P(("dom", "orb"), None),
    )
    return jax.shard_map(
        body, mesh=mesh, in_specs=placed, out_specs=P(("dom", "orb"), None), check_vma=False
    )
```

profile of v0, /device:TPU:0, one launch (start us, length us, event | category | flops | bytes accessed | tf_op | source)
XLA Modules:
  0.0 117.4 jit_solution(5434682288575688342)
XLA Ops:
  1.3 1.3 %reduce.5 = f32[48]{0:T(128)S(1)} reduce(f32[1,48]{1,0:T(1,128)} %param.10, f32[]{:T(128)} %broadcast.177), dimensions={0}, to_apply=%param.10.reduce_sub_computation.3 | reduce | bytes 388 | tf_op args[3]
  3.2 1.8 %fusion.196 = (f32[]{:T(128)}, f32[]{:T(128)}) fusion(f32[1,48,2304]{2,1,0:T(8,128)} %param.11), kind=kLoop, calls=%fused_computation.276 | loop fusion | flops 221182 | bytes 442376 | tf_op jit(solution)/shard_map/reduce_min | solution.py:39
  8.3 1.0 broadcast_multiply_fusion
  11.1 0.9 fusion.6
  13.2 1.1 fusion.15
  15.4 1.0 fusion.24
  17.6 1.0 fusion.33
  19.7 1.0 fusion.42
  21.9 1.0 fusion.51
  24.3 1.0 fusion.60
  26.5 1.0 multiply_reduce_fusion.1
  27.9 0.9 add_multiply_fusion.1.refs_0_
  28.8 37.8 %field_first.1 = (f32[12,4,2304]{2,1,0:T(4,128)}, f32[4,2304]{1,0:T(4,128)}) custom-call(f32[12,4,2304]{2,1,0:T(4,128)} %add_multiply_fusion.1.refs_0_, f32[4,2304]{1,0:T(4,128)} %refs_1_.1), custom_call_target="tpu_custom_call" | custom-call | tf_op jit(solution)/shard_map/field_first/pallas_call | solution.py:263
  70.9 0.9 fusion.76
  73.0 1.1 fusion.85
  75.2 1.0 fusion.94
  77.4 1.0 fusion.103
  79.5 1.0 fusion.112
  81.7 1.0 fusion.121
  84.1 1.0 fusion.130
  86.2 1.0 multiply_reduce_fusion
  87.6 0.9 add_multiply_fusion.refs_0_
  88.5 27.5 %field_last.1 = f32[4,2304]{1,0:T(4,128)} custom-call(f32[12,4,2304]{2,1,0:T(4,128)} %add_multiply_fusion.refs_0_, f32[4,2304]{1,0:T(4,128)} %get-tuple-element.8.refs_1_), custom_call_target="tpu_custom_call" | custom-call | tf_op jit(solution)/shard_map/field_last/pallas_call | solution.py:263
  116.0 1.4 %copy.10 = f32[4,2304]{1,0:T(4,128)} copy(f32[4,2304]{1,0:T(4,128)} %field_last.1) | data formatting | bytes 73728
  (117 shorter events, 25.0 us)
Async XLA Ops:
  0.0 8.2 %copy-start = (f32[1,2,48,2304]{3,2,1,0:T(8,128)S(1)}, f32[1,2,48,2304]{3,2,1,0:T(8,128)}, u32[]{:S(2)}) copy-start(f32[1,2,48,2304]{3,2,1,0:T(8,128)} %param.7) | copy-start | bytes 2654212
  10.1 1.0 copy-start.1
  66.6 1.0 copy-start.2
where the time goes:
time: 118 us; the launch traced here: 117 us
  Pallas kernels  65.3 us (55%)
  local copies, waits for them, and re-layouts  24.5 us (21%)
  other arithmetic  24.1 us (20%)
  between operations  3.5 us (3%)
    pallas_call x2, Pallas kernels, field_step(): pl.pallas_call(functools.partial(field_kernel, last, doms, ranks), out_sh...  65.3 us
    sub x12, other arithmetic, chebyshev(): 2.0 * (hamiltonian(current, box_potential) - center * current) / half_width  12.3 us
    slice x32, local copies, waits for them, and re-layouts, transverse_sum(): return left + right + jnp.roll(field, SIDE, -1) + jnp.roll(field, -SIDE, -1)  6.44 us
    slice x28, local copies, waits for them, and re-layouts, transverse_sum(): jnp.roll(field, SIDE - 1, -1)  6.18 us
    slice x28, local copies, waits for them, and re-layouts, transverse_sum(): jnp.roll(field, -1, -1)  6.17 us
    unnamed x8, local copies, waits for them, and re-layouts  3.42 us
    reduce_min x2, other arithmetic, chebyshev(): low_bound = jnp.min(box_potential) + CUTOFF  2.52 us

commit v1 on v0

--- a/solution.py
+++ b/solution.py
@@ -21,35 +21,6 @@
 CUTOFF = 1.5
 
 
-def transverse_sum(field):
-    cells = field.shape[-1]
-    column = jnp.arange(cells, dtype=jnp.int32) % SIDE
-    left = jnp.where(column == 0, jnp.roll(field, -(SIDE - 1), -1), jnp.roll(field, 1, -1))
-    right = jnp.where(column == SIDE - 1, jnp.roll(field, SIDE - 1, -1), jnp.roll(field, -1, -1))
-    return left + right + jnp.roll(field, SIDE, -1) + jnp.roll(field, -SIDE, -1)
-
-
-def hamiltonian(orbital_set, box_potential):
-    padded = jnp.pad(orbital_set, ((0, 0), (1, 1), (0, 0)))
-    neighbours = padded[:, 2:] + padded[:, :-2] + transverse_sum(orbital_set)
-    return 0.5 * (6.0 * orbital_set - neighbours) + box_potential[None] * orbital_set
-
-
-def chebyshev(orbital_set, box_potential):
-    low_bound = jnp.min(box_potential) + CUTOFF
-    high_bound = jnp.max(box_potential) + 6.0
-    center = 0.5 * (high_bound + low_bound)
-    half_width = 0.5 * (high_bound - low_bound)
-    previous = orbital_set
-    current = (hamiltonian(orbital_set, box_potential) - center * orbital_set) / half_width
-    for step_index in range(DEGREE - 1):
-        following = (
-            2.0 * (hamiltonian(current, box_potential) - center * current) / half_width - previous
-        )
-        previous, current = (current, following)
-    return current
-
-
 MESH = pl.DeviceIdType.MESH
 
 
@@ -64,17 +35,106 @@
     return left + right + pltpu.roll(field, SIDE, 1) + pltpu.roll(field, cells - SIDE, 1)
 
 
-def field_kernel(last, doms, ranks, *refs):
-    weighted, start = refs[:2]
-    outs = 1 if last else 2
-    outputs = refs[2 : 2 + outs]
-    (parts, near_h, near_d, work, work_d, own_pot, box_pot, sums, dom_sums) = refs[
-        2 + outs : 11 + outs
-    ]
+def filtered_density(
+    last, ranks, orbitals, factors, weight, core, ionic, scf, result, weighted,
+    iterates, diagonal, columns,
+):
+    count, box, cells = orbitals.shape
+    planes = weighted.shape[1]
+    blocks = box // 8
+    if scf is None:
+        diagonal[...] = ionic[...]
+    else:
+        for chunk in range(box // planes):
+            rows = slice(chunk * planes, (chunk + 1) * planes)
+            diagonal[rows, :] = ionic[rows, :] + scf[chunk]
+    potential = diagonal[...]
+    lowest = jnp.min(jnp.min(potential, axis=0, keepdims=True), axis=1, keepdims=True)
+    highest = jnp.max(jnp.max(potential, axis=0, keepdims=True), axis=1, keepdims=True)
+    low_bound = lowest + CUTOFF
+    high_bound = highest + 6.0
+    center = 0.5 * (high_bound + low_bound)
+    inverse = 1.0 / (0.5 * (high_bound - low_bound))
+    diagonal[...] = (2.0 * inverse) * ((3.0 - center) + potential)
+    columns[...] = lax.broadcasted_iota(jnp.int32, columns.shape, 1) % SIDE
+    edge = jnp.zeros((8, cells), jnp.float32)
+    for orbital in range(count):
+        for side in range(2):
+            iterates[side, orbital, 0:8, :] = edge
+            iterates[side, orbital, 8 + box : 16 + box, :] = edge
+        iterates[0, orbital, 8 : 8 + box, :] = orbitals[orbital]
+    sublane = lax.broadcasted_iota(jnp.int32, (8, cells), 0)
+
+    def tile(current, orbital, block, first):
+        base = pl.multiple_of(8 * block, 8)
+        middle = iterates[current, orbital, pl.ds(base + 8, 8), :]
+        below = iterates[current, orbital, pl.ds(base, 8), :]
+        above = iterates[current, orbital, pl.ds(base + 16, 8), :]
+        near = pltpu.roll(jnp.where(sublane == 7, below, middle), 1, 0)
+        near = near + pltpu.roll(jnp.where(sublane == 0, above, middle), 7, 0)
+        near = near + lane_neighbours(middle, columns[...])
+        value = diagonal[pl.ds(base, 8), :] * middle - inverse * near
+        if first:
+            value = 0.5 * value
+        else:
+            value = value - iterates[1 - current, orbital, pl.ds(base + 8, 8), :]
+        iterates[1 - current, orbital, pl.ds(base + 8, 8), :] = value
+
+    def sweep(step, first):
+        current = lax.rem(step, 2)
+
+        def at(index, carry):
+            tile(current, lax.div(index, blocks), lax.rem(index, blocks), first)
+            return carry
+
+        lax.fori_loop(0, count * blocks, at, 0)
+
+    sweep(jnp.int32(0), True)
+    lax.fori_loop(1, DEGREE, lambda step, carry: (sweep(step, False), carry)[1], 0)
+    side = DEGREE % 2
+    shares = []
+    for orbital in range(count):
+        def squares_of(block, total):
+            base = pl.multiple_of(8 * block, 8)
+            value = iterates[side, orbital, pl.ds(base + 8, 8), :]
+            value = value * value
+            for lane in range(0, cells, 128):
+                total = total + value[:, lane : lane + 128]
+            return total
+
+        total = lax.fori_loop(0, blocks, squares_of, jnp.zeros((8, 128), jnp.float32))
+        total = jnp.sum(jnp.sum(total, axis=0, keepdims=True), axis=1, keepdims=True)
+        squares = total * (1.0 / (box * cells)) + 1e-06
+        shares.append(factors[0, orbital] / squares)
+        if not last:
+            result[orbital] = iterates[side, orbital, 8 : 8 + box, :] * (
+                1.0 / jnp.sqrt(squares)
+            )
+    for block in range(blocks):
+        rows = slice(8 * block, 8 * block + 8)
+        density = core[rows, :] * (1.0 / ranks)
+        for orbital in range(count):
+            value = iterates[side, orbital, 8 + 8 * block : 16 + 8 * block, :]
+            density = density + shares[orbital] * (value * value)
+        density = density * weight[rows, :]
+        for piece in range(8 // planes):
+            weighted[block * (8 // planes) + piece] = density[
+                piece * planes : (piece + 1) * planes, :
+            ]
+
+
+def cycle_kernel(last, has_scf, doms, ranks, *refs):
+    orbitals, factors, weight, core, ionic, start = refs[:6]
+    scf = refs[6] if has_scf else None
+    refs = refs[7:] if has_scf else refs[6:]
+    outs = 1 if last else 3
+    outputs = refs[:outs]
     (
+        weighted, iterates, diagonal, columns,
+        parts, near_h, near_d, work, work_d, own_pot, box_pot, sums, dom_sums,
         part_send, part_recv, h_send, h_recv, d_send, d_recv,
         sum_send, sum_recv, dom_send, dom_recv, box_send, box_recv,
-    ) = refs[11 + outs :]
+    ) = refs[outs:]
     chunks, planes, cells = weighted.shape
     rim = BUF // planes
     reach = near_h.shape[0] // 2
@@ -106,6 +166,10 @@
         )
 
     repeat(1, everyone, greet)
+    filtered_density(
+        last, ranks, orbitals, factors, weight, core, ionic, scf,
+        None if last else outputs[2], weighted, iterates, diagonal, columns,
+    )
     pl.semaphore_wait(barrier, everyone - 1)
 
     def part_copy(k):
@@ -248,10 +312,11 @@
     repeat(1, doms, lambda k: dom_copy(k).wait_send())
 
 
-def field_step(weighted, hartree, last):
+def run_cycle(orbitals, factors, weight, core, ionic, hartree, scf, last):
     doms, ranks = lax.axis_size("dom"), lax.axis_size("orb")
-    planes, cells = hartree.shape
-    chunks = weighted.shape[0] // planes
+    count, box_planes, cells = orbitals.shape
+    planes = hartree.shape[0]
+    chunks = box_planes // planes
     reach = -(-SWEEPS // planes)
     span = 2 * reach + 1
     rows = -(-span * planes // 8) * 8
@@ -260,12 +325,22 @@
     own = jax.ShapeDtypeStruct((planes, cells), f32)
     vmem = pl.BlockSpec(memory_space=pltpu.VMEM)
     dma = pltpu.SemaphoreType.DMA
-    results = pl.pallas_call(
-        functools.partial(field_kernel, last, doms, ranks),
-        out_shape=(own,) if last else (box, own),
-        in_specs=[vmem, vmem],
-        out_specs=(vmem,) if last else (vmem, vmem),
+    operands = [orbitals, factors, weight, core, ionic, hartree]
+    if scf is not None:
+        operands.append(scf)
+    specs = [vmem] * len(operands)
+    specs[1] = pl.BlockSpec(memory_space=pltpu.SMEM)
+    shapes = (own,) if last else (box, own, jax.ShapeDtypeStruct(orbitals.shape, f32))
+    return pl.pallas_call(
+        functools.partial(cycle_kernel, last, scf is not None, doms, ranks),
+        out_shape=shapes,
+        in_specs=specs,
+        out_specs=(vmem,) * len(shapes),
         scratch_shapes=[
+            pltpu.VMEM((chunks, planes, cells), f32),
+            pltpu.VMEM((2, count, box_planes + 16, cells), f32),
+            pltpu.VMEM((box_planes, cells), f32),
+            pltpu.VMEM((8, cells), jnp.int32),
             pltpu.VMEM((2 * ranks, planes, cells), f32),
             pltpu.VMEM((span, planes, cells), f32),
             pltpu.VMEM((span, planes, cells), f32),
@@ -285,11 +360,8 @@
         compiler_params=pltpu.CompilerParams(
             collective_id=1 if last else 0, has_side_effects=True
         ),
-        name="field_last" if last else "field_first",
-    )(weighted.reshape(chunks, planes, cells), hartree)
-    if last:
-        return results[0], None
-    return results[0].reshape(chunks * planes, cells), results[1]
+        name="cycle_last" if last else "cycle_first",
+    )(*operands)
 
 
 def body(
@@ -302,22 +374,20 @@
     factors = jnp.where(orbital_rank < occupied_count[0], occupations[0], jnp.float32(0.0)) / (
         per_device * orb_count
     )
+    factors = factors.reshape(1, per_device)
     box_weight = weights[0][:, None]
-    core_share = core_density[0] / orb_count
-    ionic = external_potential[0]
     orbital_set = orbitals[0]
     hartree = hartree_guess
-    scf_box = jnp.zeros_like(ionic)
+    scf = None
     for cycle_index in range(CYCLES):
-        orbital_set = chebyshev(orbital_set, ionic + scf_box)
-        squares = jnp.mean(orbital_set * orbital_set, axis=(1, 2)) + 1e-06
-        orbital_set = orbital_set / jnp.sqrt(squares)[:, None, None]
-        density_part = jnp.sum(factors[:, None, None] * orbital_set * orbital_set, axis=0)
-        weighted = (density_part + core_share) * box_weight
         last = cycle_index + 1 == CYCLES
-        result, hartree = field_step(weighted, hartree, last)
-        scf_box = result
-    return result
+        results = run_cycle(
+            orbital_set, factors, box_weight, core_density[0], external_potential[0],
+            hartree, scf, last,
+        )
+        if last:
+            return results[0]
+        scf, hartree, orbital_set = results
 
 
 def solution(mesh):

time: 118 us -> 103 us (0.87)
  Pallas kernels: 65.3 us -> 97.9 us
  other arithmetic: 24.1 us -> 0.53 us
  local copies, waits for them, and re-layouts: 24.5 us -> 3.39 us
  between operations: 3.5 us -> 0.68 us
    pallas_call x2, Pallas kernels: 65.3 us -> 97.9 us  [run_cycle(): pl.pallas_call(functools.partial(cycle_kernel, last, scf is not None, dom...]
    slice x96 -> x0, local copies, waits for them, and re-layouts: 20.3 us -> none  [the longest x32 6.44 us: transverse_sum(): return left + right + jnp.roll(field, SIDE, -1) + jnp.roll(field, -SIDE, -1)]
    sub x12 -> x0, other arithmetic: 12.3 us -> none  [chebyshev(): 2.0 * (hamiltonian(current, box_potential) - center * current) / half_width]
    div x3 -> x0, other arithmetic: 2.89 us -> none  [the longest x2 1.84 us: chebyshev(): (hamiltonian(orbital_set, box_potential) - center * orbital_set) / half_w...]
    reduce_min x2 -> x0, other arithmetic: 2.52 us -> none  [chebyshev(): low_bound = jnp.min(box_potential) + CUTOFF]
    reduce_sum x4 -> x0, other arithmetic: 2.45 us -> none  [the longest x2 2.02 us: body(): squares = jnp.mean(orbital_set * orbital_set, axis=(1, 2)) + 1e-06]
    mul x3 -> x0, other arithmetic: 1.92 us -> none  [the longest x2 1.87 us: body(): weighted = (density_part + core_share) * box_weight]
    unnamed x1 -> x0, other arithmetic: 1.3 us -> none
where the time goes in v1:
time: 103 us; the launch traced here: 102 us
  Pallas kernels  97.9 us (95%)
  local copies, waits for them, and re-layouts  3.39 us (3%)
    pallas_call x2, Pallas kernels, run_cycle(): pl.pallas_call(functools.partial(cycle_kernel, last, scf is not None, dom...  97.9 us
    unnamed x5, local copies, waits for them, and re-layouts  2.69 us

profile of v1, /device:TPU:0, one launch (start us, length us, event | category | flops | bytes accessed | tf_op | source)
XLA Modules:
  0.0 102.5 jit_solution(14366309004512944887)
XLA Ops:
  0.7 0.0 copy-start.1
  0.7 0.6 copy-done.1
  1.3 0.5 fusion.refs_1_
  1.8 0.0 copy-start
  1.8 0.7 copy-done
  2.5 0.7 copy.8.refs_2_
  3.2 54.6 %cycle_first.1 = (f32[12,4,2304]{2,1,0:T(4,128)}, f32[4,2304]{1,0:T(4,128)}, f32[2,48,2304]{2,1,0:T(8,128)}) custom-call(f32[2,48,2304]{2,1,0:T(8,128)} %bitcast.10, f32[1,2]{1,0:T(1,128)} %fusion.refs_1_, f32[48,1]{1,0:T(8,128)} %copy.8.refs_2_, f32[48,2304]{1,0:T(8,128)} %bitcast.6, f32[48,2304]{1,0:T(8,128)} %bitcast.8, f32[4,2304]{1,0:T(4,128)} %refs_5_.1), custom_call_target="tpu_custom_call" | custom-call | tf_op jit(solution)/shard_map/cycle_first/pallas_call | solution.py:334
  57.8 43.3 %cycle_last.1 = f32[4,2304]{1,0:T(4,128)} custom-call(f32[2,48,2304]{2,1,0:T(8,128)} %get-tuple-element.8.refs_0_, f32[1,2]{1,0:T(1,128)} %fusion.refs_1_, f32[48,1]{1,0:T(8,128)} %copy.8.refs_2_, f32[48,2304]{1,0:T(8,128)} %bitcast.7, f32[48,2304]{1,0:T(8,128)} %bitcast.9, f32[4,2304]{1,0:T(4,128)} %get-tuple-element.9.refs_5_, ...), custom_call_target="tpu_custom_call" | custom-call | tf_op jit(solution)/shard_map/cycle_last/pallas_call | solution.py:334
  101.1 1.4 %copy.12 = f32[4,2304]{1,0:T(4,128)} copy(f32[4,2304]{1,0:T(4,128)} %cycle_last.1) | data formatting | bytes 73728
Async XLA Ops:
  0.7 0.7 copy-start.1
  1.8 0.7 copy-start

commit v2 on v1

--- a/solution.py
+++ b/solution.py
@@ -37,7 +37,7 @@
 
 def filtered_density(
     last, ranks, orbitals, factors, weight, core, ionic, scf, result, weighted,
-    iterates, diagonal, columns,
+    even, odd, diagonal, columns,
 ):
     count, box, cells = orbitals.shape
     planes = weighted.shape[1]
@@ -59,44 +59,54 @@
     columns[...] = lax.broadcasted_iota(jnp.int32, columns.shape, 1) % SIDE
     edge = jnp.zeros((8, cells), jnp.float32)
     for orbital in range(count):
-        for side in range(2):
-            iterates[side, orbital, 0:8, :] = edge
-            iterates[side, orbital, 8 + box : 16 + box, :] = edge
-        iterates[0, orbital, 8 : 8 + box, :] = orbitals[orbital]
+        for buffer in (even, odd):
+            buffer[orbital, 0:8, :] = edge
+            buffer[orbital, 8 + box : 16 + box, :] = edge
+        even[orbital, 8 : 8 + box, :] = orbitals[orbital]
     sublane = lax.broadcasted_iota(jnp.int32, (8, cells), 0)
 
-    def tile(current, orbital, block, first):
-        base = pl.multiple_of(8 * block, 8)
-        middle = iterates[current, orbital, pl.ds(base + 8, 8), :]
-        below = iterates[current, orbital, pl.ds(base, 8), :]
-        above = iterates[current, orbital, pl.ds(base + 16, 8), :]
-        near = pltpu.roll(jnp.where(sublane == 7, below, middle), 1, 0)
-        near = near + pltpu.roll(jnp.where(sublane == 0, above, middle), 7, 0)
-        near = near + lane_neighbours(middle, columns[...])
-        value = diagonal[pl.ds(base, 8), :] * middle - inverse * near
-        if first:
-            value = 0.5 * value
-        else:
-            value = value - iterates[1 - current, orbital, pl.ds(base + 8, 8), :]
-        iterates[1 - current, orbital, pl.ds(base + 8, 8), :] = value
-
-    def sweep(step, first):
-        current = lax.rem(step, 2)
-
-        def at(index, carry):
-            tile(current, lax.div(index, blocks), lax.rem(index, blocks), first)
+    def sweep(source, target, first):
+        def at(block, carry):
+            base = pl.multiple_of(8 * block, 8)
+            middle_rows = pl.ds(base + 8, 8)
+            scale = diagonal[pl.ds(base, 8), :]
+            column = columns[...]
+            values = []
+            for orbital in range(count):
+                middle = source[orbital, middle_rows, :]
+                below = source[orbital, pl.ds(base, 8), :]
+                above = source[orbital, pl.ds(base + 16, 8), :]
+                near = pltpu.roll(jnp.where(sublane == 7, below, middle), 1, 0)
+                near = near + pltpu.roll(jnp.where(sublane == 0, above, middle), 7, 0)
+                near = near + lane_neighbours(middle, column)
+                value = scale * middle - inverse * near
+                if first:
+                    value = 0.5 * value
+                else:
+                    value = value - target[orbital, middle_rows, :]
+                values.append(value)
+            for orbital in range(count):
+                target[orbital, middle_rows, :] = values[orbital]
             return carry
 
-        lax.fori_loop(0, count * blocks, at, 0)
-
-    sweep(jnp.int32(0), True)
-    lax.fori_loop(1, DEGREE, lambda step, carry: (sweep(step, False), carry)[1], 0)
-    side = DEGREE % 2
+        lax.fori_loop(0, blocks, at, 0, unroll=True)
+
+    sweep(even, odd, True)
+
+    def two_sweeps(step, carry):
+        sweep(odd, even, False)
+        sweep(even, odd, False)
+        return carry
+
+    lax.fori_loop(0, (DEGREE - 1) // 2, two_sweeps, 0)
+    if DEGREE % 2 == 0:
+        sweep(odd, even, False)
+    final = even if DEGREE % 2 == 0 else odd
     shares = []
     for orbital in range(count):
         def squares_of(block, total):
             base = pl.multiple_of(8 * block, 8)
-            value = iterates[side, orbital, pl.ds(base + 8, 8), :]
+            value = final[orbital, pl.ds(base + 8, 8), :]
             value = value * value
             for lane in range(0, cells, 128):
                 total = total + value[:, lane : lane + 128]
@@ -107,14 +117,14 @@
         squares = total * (1.0 / (box * cells)) + 1e-06
         shares.append(factors[0, orbital] / squares)
         if not last:
-            result[orbital] = iterates[side, orbital, 8 : 8 + box, :] * (
+            result[orbital] = final[orbital, 8 : 8 + box, :] * (
                 1.0 / jnp.sqrt(squares)
             )
     for block in range(blocks):
         rows = slice(8 * block, 8 * block + 8)
         density = core[rows, :] * (1.0 / ranks)
         for orbital in range(count):
-            value = iterates[side, orbital, 8 + 8 * block : 16 + 8 * block, :]
+            value = final[orbital, 8 + 8 * block : 16 + 8 * block, :]
             density = density + shares[orbital] * (value * value)
         density = density * weight[rows, :]
         for piece in range(8 // planes):
@@ -130,7 +140,7 @@
     outs = 1 if last else 3
     outputs = refs[:outs]
     (
-        weighted, iterates, diagonal, columns,
+        weighted, even, odd, diagonal, columns,
         parts, near_h, near_d, work, work_d, own_pot, box_pot, sums, dom_sums,
         part_send, part_recv, h_send, h_recv, d_send, d_recv,
         sum_send, sum_recv, dom_send, dom_recv, box_send, box_recv,
@@ -168,7 +178,7 @@
     repeat(1, everyone, greet)
     filtered_density(
         last, ranks, orbitals, factors, weight, core, ionic, scf,
-        None if last else outputs[2], weighted, iterates, diagonal, columns,
+        None if last else outputs[2], weighted, even, odd, diagonal, columns,
     )
     pl.semaphore_wait(barrier, everyone - 1)
 
@@ -338,7 +348,8 @@
         out_specs=(vmem,) * len(shapes),
         scratch_shapes=[
             pltpu.VMEM((chunks, planes, cells), f32),
-            pltpu.VMEM((2, count, box_planes + 16, cells), f32),
+            pltpu.VMEM((count, box_planes + 16, cells), f32),
+            pltpu.VMEM((count, box_planes + 16, cells), f32),
             pltpu.VMEM((box_planes, cells), f32),
             pltpu.VMEM((8, cells), jnp.int32),
             pltpu.VMEM((2 * ranks, planes, cells), f32),

time: 103 us -> 91.9 us (0.89)
  Pallas kernels: 97.9 us -> 87 us
    pallas_call x2, Pallas kernels: 97.9 us -> 87 us  [run_cycle(): pl.pallas_call(functools.partial(cycle_kernel, last, scf is not None, dom...]
where the time goes in v2:
time: 91.9 us; the launch traced here: 91.6 us
  Pallas kernels  87 us (95%)
  local copies, waits for them, and re-layouts  3.39 us (4%)
    pallas_call x2, Pallas kernels, run_cycle(): pl.pallas_call(functools.partial(cycle_kernel, last, scf is not None, dom...  87 us
    unnamed x5, local copies, waits for them, and re-layouts  2.69 us

profile of v2, /device:TPU:0, one launch (start us, length us, event | category | flops | bytes accessed | tf_op | source)
XLA Modules:
  0.0 91.6 jit_solution(14265688380679447434)
XLA Ops:
  0.7 0.0 copy-start.1
  0.7 0.6 copy-done.1
  1.3 0.5 fusion.refs_1_
  1.8 0.0 copy-start
  1.8 0.7 copy-done
  2.5 0.7 copy.8.refs_2_
  3.2 49.3 %cycle_first.1 = (f32[12,4,2304]{2,1,0:T(4,128)}, f32[4,2304]{1,0:T(4,128)}, f32[2,48,2304]{2,1,0:T(8,128)}) custom-call(f32[2,48,2304]{2,1,0:T(8,128)} %bitcast.10, f32[1,2]{1,0:T(1,128)} %fusion.refs_1_, f32[48,1]{1,0:T(8,128)} %copy.8.refs_2_, f32[48,2304]{1,0:T(8,128)} %bitcast.6, f32[48,2304]{1,0:T(8,128)} %bitcast.8, f32[4,2304]{1,0:T(4,128)} %refs_5_.1), custom_call_target="tpu_custom_call" | custom-call | tf_op jit(solution)/shard_map/cycle_first/pallas_call | solution.py:344
  52.5 37.7 %cycle_last.1 = f32[4,2304]{1,0:T(4,128)} custom-call(f32[2,48,2304]{2,1,0:T(8,128)} %get-tuple-element.8.refs_0_, f32[1,2]{1,0:T(1,128)} %fusion.refs_1_, f32[48,1]{1,0:T(8,128)} %copy.8.refs_2_, f32[48,2304]{1,0:T(8,128)} %bitcast.7, f32[48,2304]{1,0:T(8,128)} %bitcast.9, f32[4,2304]{1,0:T(4,128)} %get-tuple-element.9.refs_5_, ...), custom_call_target="tpu_custom_call" | custom-call | tf_op jit(solution)/shard_map/cycle_last/pallas_call | solution.py:344
  90.2 1.4 %copy.12 = f32[4,2304]{1,0:T(4,128)} copy(f32[4,2304]{1,0:T(4,128)} %cycle_last.1) | data formatting | bytes 73728
Async XLA Ops:
  0.7 0.7 copy-start.1
  1.8 0.7 copy-start
